TPU v7x, 32 devices: a 4x4x1 block of a 4x4x8 slice. The times are simulated.
32 devices in a mesh: dp: 1 (over z), cp: 32 (over y, x, core).
Axes of the slice: x: 4, y: 4, z: 1, core: 2. Of those that a mesh axis runs over, the one named last changes fastest.
The devices are a block of a 4x4x8 slice.
Arguments:
- x_in: bfloat16 [4096, 4096], P(('dp', 'cp'))
- dy_in: bfloat16 [4096, 4096], P(('dp', 'cp'))
- w_q: bfloat16 [4096, 4096], replicated
- w_k: bfloat16 [4096, 1024], replicated
- w_v: bfloat16 [4096, 1024], replicated
- w_o: bfloat16 [4096, 4096], replicated
Outputs:
- output 1: bfloat16 [4096, 4096], P(('dp', 'cp'))
- output 2: bfloat16 [4096, 4096], P(('dp', 'cp'))
All inputs are finite; a program needn't handle non-finite values.
Results may differ from a plain program's by a relative error of at most 0.0107204.
Values are sent between devices in bfloat16 or wider.
A program may use at most 768 MiB of HBM per device.

v0:
```python
import jax
import jax.numpy as jnp
from jax import lax
from jax.sharding import PartitionSpec as P

HEAD_DIM = 128
SCORE_LIMIT = 8388608


def block_rows(n_rows, n_heads, n_keys):
    blk_rows = n_rows
    for step_idx in range(30):
        if blk_rows % 2 == 0 and blk_rows > 8 and blk_rows * n_heads * n_keys > SCORE_LIMIT:
            blk_rows = blk_rows // 2
    return blk_rows


def split_rows(array_in, blk_rows):
    return array_in.reshape((array_in.shape[0] // blk_rows, blk_rows) + array_in.shape[1:])


def project(rows_in, weight):
    return jnp.dot(rows_in, weight, preferred_element_type=jnp.float32).astype(jnp.bfloat16)


def attend_forward(q_loc, k_all, v_all, blk_rows):
    n_rows, kv_heads, q_group, head_dim = q_loc.shape
    score_scale = head_dim ** -0.5

    def one_block(q_blk):
        scores = jnp.einsum("thjd,uhd->thju", q_blk, k_all, preferred_element_type=jnp.float32) * score_scale
        lse_blk = jax.nn.logsumexp(scores, axis=-1, keepdims=True)
        prob_bf = jnp.exp(scores - lse_blk).astype(jnp.bfloat16)
        out_blk = jnp.einsum("thju,uhd->thjd", prob_bf, v_all, preferred_element_type=jnp.float32).astype(jnp.bfloat16)
        return out_blk, lse_blk

    out_blocks, lse_blocks = lax.map(one_block, split_rows(q_loc, blk_rows))
    return out_blocks.reshape(n_rows, kv_heads, q_group, head_dim), lse_blocks.reshape(n_rows, kv_heads, q_group, 1)


def attend_backward(q_loc, k_all, v_all, lse_loc, delta_loc, do_loc, blk_rows):
    n_rows, kv_heads, q_group, head_dim = q_loc.shape
    score_scale = head_dim ** -0.5

    def one_block(acc_pair, block_in):
        dk_acc, dv_acc = acc_pair
        q_blk, do_blk, lse_blk, delta_blk = block_in
        scores = jnp.einsum("thjd,uhd->thju", q_blk, k_all, preferred_element_type=jnp.float32) * score_scale
        prob_bf = jnp.exp(scores - lse_blk).astype(jnp.bfloat16)
        dprob = jnp.einsum("thjd,uhd->thju", do_blk, v_all, preferred_element_type=jnp.float32)
        dscore = (prob_bf.astype(jnp.float32) * (dprob - delta_blk)).astype(jnp.bfloat16)
        dq_blk = (jnp.einsum("thju,uhd->thjd", dscore, k_all, preferred_element_type=jnp.float32) * score_scale).astype(jnp.bfloat16)
        dk_acc = dk_acc + jnp.einsum("thju,thjd->uhd", dscore, q_blk, preferred_element_type=jnp.float32) * score_scale
        dv_acc = dv_acc + jnp.einsum("thju,thjd->uhd", prob_bf, do_blk, preferred_element_type=jnp.float32)
        return (dk_acc, dv_acc), dq_blk

    zero_acc = jnp.zeros(k_all.shape, jnp.float32)
    blocks_in = (split_rows(q_loc, blk_rows), split_rows(do_loc, blk_rows), split_rows(lse_loc, blk_rows), split_rows(delta_loc, blk_rows))
    acc_final, dq_blocks = lax.scan(one_block, (zero_acc, zero_acc), blocks_in)
    return dq_blocks.reshape(n_rows, kv_heads * q_group * head_dim), acc_final[0], acc_final[1]


def solution(mesh):
    n_group = mesh.shape["cp"]
    row_spec = P(("dp", "cp"), None)
    full_spec = P(None, None)

    def local_body(x_loc, dy_loc, w_q, w_k, w_v, w_o):
        n_rows = x_loc.shape[0]
        q_heads = w_q.shape[1] // HEAD_DIM
        kv_heads = w_k.shape[1] // HEAD_DIM
        q_group = q_heads // kv_heads
        blk_rows = block_rows(n_rows, q_heads, n_rows * n_group)
        q_loc = project(x_loc, w_q).reshape(n_rows, kv_heads, q_group, HEAD_DIM)
        k_loc = project(x_loc, w_k).reshape(n_rows, kv_heads, HEAD_DIM)
        v_loc = project(x_loc, w_v).reshape(n_rows, kv_heads, HEAD_DIM)
        k_all = lax.all_gather(k_loc, "cp", axis=0, tiled=True)
        v_all = lax.all_gather(v_loc, "cp", axis=0, tiled=True)
        out_loc, lse_loc = attend_forward(q_loc, k_all, v_all, blk_rows)
        y_loc = project(out_loc.reshape(n_rows, q_heads * HEAD_DIM), w_o)
        do_loc = jnp.einsum("te,ce->tc", dy_loc, w_o, preferred_element_type=jnp.float32).astype(jnp.bfloat16).reshape(n_rows, kv_heads, q_group, HEAD_DIM)
        delta_loc = jnp.einsum("thjd,thjd->thj", do_loc, out_loc, preferred_element_type=jnp.float32)[..., None]
        dq_flat, dk_part, dv_part = attend_backward(q_loc, k_all, v_all, lse_loc, delta_loc, do_loc, blk_rows)
        dk_own = lax.psum_scatter(dk_part, "cp", scatter_dimension=0, tiled=True).astype(jnp.bfloat16).reshape(n_rows, kv_heads * HEAD_DIM)
        dv_own = lax.psum_scatter(dv_part, "cp", scatter_dimension=0, tiled=True).astype(jnp.bfloat16).reshape(n_rows, kv_heads * HEAD_DIM)
        dx_acc = (jnp.einsum("tc,ec->te", dq_flat, w_q, preferred_element_type=jnp.float32)
                  + jnp.einsum("tc,ec->te", dk_own, w_k, preferred_element_type=jnp.float32)
                  + jnp.einsum("tc,ec->te", dv_own, w_v, preferred_element_type=jnp.float32))
        return y_loc, dx_acc.astype(jnp.bfloat16)

    return jax.shard_map(local_body, mesh=mesh,
                         in_specs=(row_spec, row_spec, full_spec, full_spec, full_spec, full_spec),
                         out_specs=(row_spec, row_spec), check_vma=False)
```

profile of v0, /device:TPU:97, one launch (start us, length us, event | category | flops | bytes accessed | tf_op | source)
XLA Modules:
  0.0 609.8 jit_solution(7244677508651661784)
XLA Ops:
  19.5 16.0 %convolution_convert_fusion = bf16[128,4096]{1,0:T(8,128)(2,1)S(1)} fusion(bf16[128,4096]{1,0:T(8,128)(2,1)S(1)} %copy-done.5, bf16[4096,4096]{1,0:T(8,128)(2,1)} %param.15), kind=kOutput, calls=%fused_computation.56 | convolution fusion | flops 4295491584 | bytes 35651584 | tf_op jit(solution)/shard_map/te,ce->tc/dot_general | solution.py:81
  37.8 13.0 %convolution_convert_fusion.2 = bf16[128,4096]{1,0:T(8,128)(2,1)S(1)} fusion(bf16[128,4096]{1,0:T(8,128)(2,1)S(1)} %copy-done, bf16[4096,4096]{1,0:T(8,128)(2,1)} %param.12), kind=kOutput, calls=%fused_computation.58 | convolution fusion | flops 4295491584 | bytes 35651584 | tf_op jit(solution)/shard_map/dot_general | solution.py:23
  65.7 49.0 %all-gather.5.cloned.1.call-done = bf16[4096,8,128]{2,0,1:T(8,128)(2,1)} async-done(((bf16[128,8,128]{2,0,1:T(8,128)(2,1)}), bf16[4096,8,128]{2,0,1:T(8,128)(2,1)}) %all-gather.5.cloned.1.call-update) | async-done | bytes 8388624 | tf_op jit(solution)/shard_map/all_gather | solution.py:78
  114.7 95.7 %while.27 = (s32[]{:T(128)}, bf16[2,64,8,4,128]{4,1,3,2,0:T(8,128)(2,1)}, f32[2,64,8,4,1]{1,3,2,4,0:T(4,128)S(1)}, bf16[2,64,8,4,128]{4,1,3,2,0:T(8,128)(2,1)S(1...) while((s32[]{:T(128)}, bf16[2,64,8,4,128]{4,1,3,2,0:T(8,128)(2,1)}, ...), condition=%wide.region_3.4_spmd, body=%wide.region_0.3_spmd.sunk | while | flops 4362354688 | bytes 118612560 | solution.py:37
  115.1 16.5 %bitcast_reduce_fusion.2 = (f32[64,8,4]{0,2,1:T(4,128)S(1)}, f32[8,64,4,4096]{3,1,2,0:T(8,128)}) fusion(bf16[4096,8,128]{2,0,1:T(8,128)(2,1)} %get-tuple-element.319, bf16[2,64,8,4,128]{4,1,3,2,0:T(8,128)(2,1)S(1)} %get-tuple-element.318, s32[]{:T(128)} %get-tuple-element.308), kind=kOutput, calls=%fused_computation.2.clone.1 | convolution fusion | flops 2164258816 | bytes 42475524 | tf_op jit(solution)/shard_map/while/body/eval_jaxpr/thjd,uhd->thju/dot_general | solution.py:31
  131.6 14.0 %fusion.98 = f32[64,8,4]{0,2,1:T(4,128)S(1)} fusion(f32[8,64,4,4096]{3,1,2,0:T(8,128)} %get-tuple-element.287, f32[64,8,4]{0,2,1:T(4,128)S(1)} %is-finite_select_fusion.3), kind=kLoop, calls=%fused_computation.4.clone.1 | loop fusion | flops 25163776 | bytes 33570816 | tf_op jit(solution)/shard_map/while/body/eval_jaxpr/reduce_sum | solution.py:32
  145.7 17.0 %fusion.100 = bf16[2,64,8,4,128]{4,1,3,2,0:T(8,128)(2,1)} fusion(bf16[2,64,8,4,128]{4,1,3,2,0:T(8,128)(2,1)} %get-tuple-element.309, s32[]{:T(128)} %get-tuple-element.308, bf16[4096,8,128]{2,0,1:T(8,128)(2,1)} %get-tuple-element.320, f32[8,64,4,4096]{3,1,2,0:T(8,128)} %get-tuple-element.287, f32[64,8,4]{0,2,1:T(4,128)S(1)} %fusion.99), kind=kOutput, calls=%fused_computation.15.clone.1 | convolution fusion | flops 2172911616 | bytes 42476032 | tf_op jit(solution)/shard_map/while/body/eval_jaxpr/thju,uhd->thjd/dot_general | solution.py:34
  162.7 16.5 %bitcast_reduce_fusion.2 = (f32[64,8,4]{0,2,1:T(4,128)S(1)}, f32[8,64,4,4096]{3,1,2,0:T(8,128)}) fusion(bf16[4096,8,128]{2,0,1:T(8,128)(2,1)} %get-tuple-element.319, bf16[2,64,8,4,128]{4,1,3,2,0:T(8,128)(2,1)S(1)} %get-tuple-element.318, s32[]{:T(128)} %get-tuple-element.308), kind=kOutput, calls=%fused_computation.2.clone.1 | convolution fusion | flops 2164258816 | bytes 42475524 | tf_op jit(solution)/shard_map/while/body/eval_jaxpr/thjd,uhd->thju/dot_general | solution.py:31
  179.3 14.0 %fusion.98 = f32[64,8,4]{0,2,1:T(4,128)S(1)} fusion(f32[8,64,4,4096]{3,1,2,0:T(8,128)} %get-tuple-element.287, f32[64,8,4]{0,2,1:T(4,128)S(1)} %is-finite_select_fusion.3), kind=kLoop, calls=%fused_computation.4.clone.1 | loop fusion | flops 25163776 | bytes 33570816 | tf_op jit(solution)/shard_map/while/body/eval_jaxpr/reduce_sum | solution.py:32
  193.3 17.0 %fusion.100 = bf16[2,64,8,4,128]{4,1,3,2,0:T(8,128)(2,1)} fusion(bf16[2,64,8,4,128]{4,1,3,2,0:T(8,128)(2,1)} %get-tuple-element.309, s32[]{:T(128)} %get-tuple-element.308, bf16[4096,8,128]{2,0,1:T(8,128)(2,1)} %get-tuple-element.320, f32[8,64,4,4096]{3,1,2,0:T(8,128)} %get-tuple-element.287, f32[64,8,4]{0,2,1:T(4,128)S(1)} %fusion.99), kind=kOutput, calls=%fused_computation.15.clone.1 | convolution fusion | flops 2172911616 | bytes 42476032 | tf_op jit(solution)/shard_map/while/body/eval_jaxpr/thju,uhd->thjd/dot_general | solution.py:34
  214.7 163.5 %while.28 = (s32[]{:T(128)}, f32[4096,8,128]{0,2,1:T(8,128)}, f32[4096,8,128]{0,2,1:T(8,128)}, bf16[2,64,8,4,128]{4,3,2,1,0:T(4,128)(2,1)}, bf16[2,64,8,4,128]{4...) while((s32[]{:T(128)}, f32[4096,8,128]{0,2,1:T(8,128)}, ...), condition=%wide.region_5.6_spmd.clone, body=%wide.region_4.5_spmd.clone.sunk | while | flops 10817634304 | bytes 206102736 | solution.py:59
  214.9 12.3 %fusion.110 = bf16[64,8,4,4096]{3,0,2,1:T(8,128)(2,1)} fusion(f32[64,8,4]{0,2,1:T(4,128)S(1)} %get-tuple-element.299, bf16[4096,8,128]{2,0,1:T(8,128)(2,1)} %get-tuple-element.351, bf16[2,64,8,4,128]{4,1,3,2,0:T(8,128)(2,1)S(1)} %get-tuple-element.350, s32[]{:T(128)} %get-tuple-element.334), kind=kOutput, calls=%fused_computation.31.clone.1 | convolution fusion | flops 2172649472 | bytes 25706500 | tf_op jit(solution)/shard_map/while/body/eval_jaxpr/thjd,uhd->thju/dot_general | solution.py:48
  227.4 19.6 %fusion.111 = bf16[64,8,4,4096]{3,0,2,1:T(8,128)(2,1)} fusion(bf16[64,8,4,4096]{3,0,2,1:T(8,128)(2,1)} %fusion.110, f32[64,8,4]{0,2,1:T(4,128)S(1)} %get-tuple-element.300, bf16[4096,8,128]{2,0,1:T(8,128)(2,1)} %get-tuple-element.354, bf16[1,64,8,4,128]{4,3,2,1,0:T(4,128)(2,1)S(1)} %constant_dynamic-slice_fusion.2), kind=kOutput, calls=%fused_computation.28.clone.1 | convolution fusion | flops 2181038080 | bytes 42475520 | tf_op jit(solution)/shard_map/while/body/eval_jaxpr/thjd,uhd->thju/dot_general | solution.py:50
  247.0 15.9 %bitcast_add_fusion.4 = f32[4096,8,128]{0,2,1:T(8,128)} fusion(f32[4096,8,128]{0,2,1:T(8,128)} %get-tuple-element.335, bf16[64,8,4,4096]{3,0,2,1:T(8,128)(2,1)} %fusion.111, pred[]{:T(512)S(6)} %compare.3, bf16[2,64,8,4,128]{4,1,3,2,0:T(8,128)(2,1)S(1)} %get-tuple-element.350, s32[]{:T(128)} %get-tuple-element.334), kind=kOutput, calls=%fused_computation.33.clone.1 | convolution fusion | flops 2160066560 | bytes 50855940 | tf_op jit(solution)/shard_map/while/body/eval_jaxpr/thju,thjd->uhd/dot_general | solution.py:53
  262.8 12.8 %fusion.112 = bf16[1,64,8,4,128]{4,1,3,2,0:T(8,128)(2,1)S(1)} fusion(bf16[64,8,4,4096]{3,0,2,1:T(8,128)(2,1)} %fusion.111, bf16[4096,8,128]{2,0,1:T(8,128)(2,1)} %get-tuple-element.351), kind=kOutput, calls=%fused_computation.41.clone.1 | convolution fusion | flops 2148007936 | bytes 25690112 | tf_op jit(solution)/shard_map/while/body/eval_jaxpr/thju,uhd->thjd/dot_general | solution.py:52
  277.1 14.6 %bitcast_add_fusion.5 = f32[4096,8,128]{0,2,1:T(8,128)} fusion(f32[4096,8,128]{0,2,1:T(8,128)} %get-tuple-element.336, bf16[64,8,4,4096]{3,0,2,1:T(8,128)(2,1)} %fusion.110, pred[]{:T(512)S(6)} %compare.3, bf16[1,64,8,4,128]{4,3,2,1,0:T(4,128)(2,1)S(1)} %constant_dynamic-slice_fusion.2), kind=kOutput, calls=%fused_computation.32.clone.1 | convolution fusion | flops 2155872256 | bytes 50855936 | tf_op jit(solution)/shard_map/while/body/eval_jaxpr/thju,thjd->uhd/dot_general | solution.py:54
  304.1 19.6 %fusion.111 = bf16[64,8,4,4096]{3,0,2,1:T(8,128)(2,1)} fusion(bf16[64,8,4,4096]{3,0,2,1:T(8,128)(2,1)} %fusion.110, f32[64,8,4]{0,2,1:T(4,128)S(1)} %get-tuple-element.300, bf16[4096,8,128]{2,0,1:T(8,128)(2,1)} %get-tuple-element.354, bf16[1,64,8,4,128]{4,3,2,1,0:T(4,128)(2,1)S(1)} %constant_dynamic-slice_fusion.2), kind=kOutput, calls=%fused_computation.28.clone.1 | convolution fusion | flops 2181038080 | bytes 42475520 | tf_op jit(solution)/shard_map/while/body/eval_jaxpr/thjd,uhd->thju/dot_general | solution.py:50
  323.7 20.7 %bitcast_add_fusion.4 = f32[4096,8,128]{0,2,1:T(8,128)} fusion(f32[4096,8,128]{0,2,1:T(8,128)} %get-tuple-element.335, bf16[64,8,4,4096]{3,0,2,1:T(8,128)(2,1)} %fusion.111, pred[]{:T(512)S(6)} %compare.3, bf16[2,64,8,4,128]{4,1,3,2,0:T(8,128)(2,1)S(1)} %get-tuple-element.350, s32[]{:T(128)} %get-tuple-element.334), kind=kOutput, calls=%fused_computation.33.clone.1 | convolution fusion | flops 2160066560 | bytes 50855940 | tf_op jit(solution)/shard_map/while/body/eval_jaxpr/thju,thjd->uhd/dot_general | solution.py:53
  344.4 12.8 %fusion.112 = bf16[1,64,8,4,128]{4,1,3,2,0:T(8,128)(2,1)S(1)} fusion(bf16[64,8,4,4096]{3,0,2,1:T(8,128)(2,1)} %fusion.111, bf16[4096,8,128]{2,0,1:T(8,128)(2,1)} %get-tuple-element.351), kind=kOutput, calls=%fused_computation.41.clone.1 | convolution fusion | flops 2148007936 | bytes 25690112 | tf_op jit(solution)/shard_map/while/body/eval_jaxpr/thju,uhd->thjd/dot_general | solution.py:52
  358.6 19.4 %bitcast_add_fusion.5 = f32[4096,8,128]{0,2,1:T(8,128)} fusion(f32[4096,8,128]{0,2,1:T(8,128)} %get-tuple-element.336, bf16[64,8,4,4096]{3,0,2,1:T(8,128)(2,1)} %fusion.110, pred[]{:T(512)S(6)} %compare.3, bf16[1,64,8,4,128]{4,3,2,1,0:T(4,128)(2,1)S(1)} %constant_dynamic-slice_fusion.2), kind=kOutput, calls=%fused_computation.32.clone.1 | convolution fusion | flops 2155872256 | bytes 50855936 | tf_op jit(solution)/shard_map/while/body/eval_jaxpr/thju,thjd->uhd/dot_general | solution.py:54
  382.7 16.0 %fusion.59 = f32[128,4096]{1,0:T(8,128)S(1)} fusion(bf16[128,4096]{1,0:T(8,128)(2,1)S(1)} %reshape.72, bf16[4096,4096]{1,0:T(8,128)(2,1)} %param.12), kind=kOutput, calls=%fused_computation.66 | convolution fusion | flops 4294967296 | bytes 36700160 | tf_op jit(solution)/shard_map/tc,ec->te/dot_general | solution.py:86
  398.7 14.1 %convolution_convert_fusion.1 = bf16[128,4096]{1,0:T(8,128)(2,1)} fusion(bf16[128,4096]{1,0:T(8,128)(2,1)S(1)} %copy-done.3, bf16[4096,4096]{1,0:T(8,128)(2,1)} %param.15), kind=kOutput, calls=%fused_computation.57 | convolution fusion | flops 4295491584 | bytes 35651584 | tf_op jit(solution)/shard_map/dot_general | solution.py:23
  412.8 70.6 %reduce-scatter.3.cloned.1.call-done = f32[128,8,128]{0,2,1:T(8,128)} async-done(((f32[4096,8,128]{0,2,1:T(8,128)}), f32[128,8,128]{0,2,1:T(8,128)}) %reduce-scatter.3.cloned.1.call-update) | async-done | bytes 524304 | tf_op jit(solution)/shard_map/reduce_scatter | solution.py:84
  492.1 101.8 %reduce-scatter.5.cloned.1.call-done = f32[128,8,128]{0,2,1:T(8,128)} async-done(((f32[4096,8,128]{0,2,1:T(8,128)}), f32[128,8,128]{0,2,1:T(8,128)}) %reduce-scatter.5.cloned.1.call-update) | async-done | bytes 524304 | tf_op jit(solution)/shard_map/reduce_scatter | solution.py:85
  (68 shorter events, 71.3 us)
Async XLA Ops:
  7.2 1.2 copy-start
  7.2 12.3 %copy-start.5 = (bf16[128,4096]{1,0:T(8,128)(2,1)S(1)}, bf16[128,4096]{1,0:T(8,128)(2,1)}, u32[]{:S(2)}) copy-start(bf16[128,4096]{1,0:T(8,128)(2,1)} %param.11) | copy-start | bytes 3145732
  7.2 58.4 %all-gather.3.cloned.1.call-start = ((), (), s32[]{:S(2)}) async-start(), calls=%async_computation.2 | async-start | bytes 8650752 | tf_op jit(solution)/shard_map/all_gather | solution.py:77
  13.9 100.8 %all-gather.5.cloned.1.call-start = ((), (), s32[]{:S(2)}) async-start(), calls=%async_computation.3 | async-start | bytes 8650752 | tf_op jit(solution)/shard_map/all_gather | solution.py:78
  19.4 464.0 %reduce-scatter.3.cloned.1.call-start = ((), (), s32[]{:S(2)}) async-start(), calls=%async_computation.4 | async-start | bytes 17301504 | tf_op jit(solution)/shard_map/reduce_scatter | solution.py:84
  114.7 100.0 %copy-start.2 = (bf16[2,64,8,4,128]{4,3,2,1,0:T(4,128)(2,1)S(1)}, bf16[2,64,8,4,128]{4,3,2,1,0:T(4,128)(2,1)}, u32[]{:S(2)}) copy-start(bf16[2,64,8,4,128]{4,3,2,1,0:T(4,128)(2,1)} %reshape_reshape.12) | copy-start | bytes 3145732
  262.8 12.8 %copy-start.6 = (bf16[2,64,8,4,128]{4,3,2,1,0:T(4,128)(2,1)S(1)}, bf16[2,64,8,4,128]{4,3,2,1,0:T(4,128)(2,1)}, u32[]{:S(2)}) copy-start(bf16[2,64,8,4,128]{4,3,2,1,0:T(4,128)(2,1)} %get-tuple-element.337) | copy-start | bytes 3145732 | tf_op jit(solution)/shard_map/while
  276.1 1.0 copy-start.7
  344.4 12.8 %copy-start.6 = (bf16[2,64,8,4,128]{4,3,2,1,0:T(4,128)(2,1)S(1)}, bf16[2,64,8,4,128]{4,3,2,1,0:T(4,128)(2,1)}, u32[]{:S(2)}) copy-start(bf16[2,64,8,4,128]{4,3,2,1,0:T(4,128)(2,1)} %get-tuple-element.337) | copy-start | bytes 3145732 | tf_op jit(solution)/shard_map/while
  357.6 1.0 copy-start.7
  378.2 1.2 copy-start.4
  378.2 2.0 copy-start.8
  378.3 215.6 %reduce-scatter.5.cloned.1.call-start = ((), (), s32[]{:S(2)}) async-start(), calls=%async_computation.5 | async-start | bytes 17301504 | tf_op jit(solution)/shard_map/reduce_scatter | solution.py:85
  382.7 16.0 %copy-start.3 = (bf16[128,4096]{1,0:T(8,128)(2,1)S(1)}, bf16[128,4096]{1,0:T(8,128)(2,1)}, u32[]{:S(2)}) copy-start(bf16[128,4096]{1,0:T(8,128)(2,1)} %reshape_reshape.11) | copy-start | bytes 3145732
  398.7 204.1 %copy-start.1 = (bf16[128,4096]{1,0:T(8,128)(2,1)S(1)}, bf16[128,4096]{1,0:T(8,128)(2,1)}, u32[]{:S(2)}) copy-start(bf16[128,4096]{1,0:T(8,128)(2,1)} %param.10) | copy-start | bytes 3145732
Sparse Core Ops, SparseCore 0:
  14.0 51.6 all-gather.2
  67.8 46.8 all-gather.4
  378.4 104.9 reduce-scatter.2
  487.0 106.8 reduce-scatter.4
where the time goes:
time: 618 us; the launch traced here: 610 us
  matrix products  311 us (50%)
  waiting for transfers between devices  234 us (38%)
  other arithmetic  34.5 us (6%)
  local copies, waits for them, and re-layouts  15.1 us (2%)
  between operations  14.4 us (2%)
    reduce_scatter x1, waiting for transfers between devices, local_body(): lax.psum_scatter(dv_part, 'cp', scatter_dimension=0, tiled=True)  102 us
    reduce_scatter x1, waiting for transfers between devices, local_body(): lax.psum_scatter(dk_part, 'cp', scatter_dimension=0, tiled=True)  70.6 us
    dot_general x4, matrix products, one_block(): jnp.einsum('thjd,uhd->thju', q_blk, k_all, preferred_element_type=jnp.flo...  57.6 us
    all_gather x1, waiting for transfers between devices, local_body(): v_all = lax.all_gather(v_loc, 'cp', axis=0, tiled=True)  49 us
    dot_general x2, matrix products, one_block(): jnp.einsum('thjd,uhd->thju', do_blk, v_all, preferred_element_type=jnp.fl...  39.2 us
    dot_general x2, matrix products, one_block(): jnp.einsum('thju,thjd->uhd', dscore, q_blk, preferred_element_type=jnp.fl...  36.5 us
    dot_general x4, matrix products, project(): jnp.dot(rows_in, weight, preferred_element_type=jnp.float32)  36.4 us
    dot_general x2, matrix products, one_block(): jnp.einsum('thju,uhd->thjd', prob_bf, v_all, preferred_element_type=jnp.f...  34 us
  transfers between devices with their start and end apart: 4, of which 4 were waited for; matrix products, arithmetic and copies ran while one was open for 13% of the time, Pallas kernels for 0%

commit v1 on v0

v1 whole, which is shorter than its diff:
```python
import functools

import jax
import jax.numpy as jnp
from jax import lax
from jax.experimental import pallas as pl
from jax.experimental.pallas import tpu as pltpu
from jax.sharding import PartitionSpec as P

HEAD_DIM = 128
LOG2E = 1.4426950408889634
N_SLOT = 4
BQ_ROWS = 512
UC_ROWS = 512
VMEM_BYTES = 62 * 1024 * 1024
MESH_ID = pl.DeviceIdType.MESH
BF = jnp.bfloat16
F32 = jnp.float32
NT = (((1,), (1,)), ((), ()))
NN = (((1,), (0,)), ((), ()))


def mm(a, b, dims=NN):
    return lax.dot_general(a, b, dims, preferred_element_type=F32)


def aligned(start, size):
    return pl.ds(pl.multiple_of(start, size), size)


def entry_barrier(seq_id, head_id, n_seq, n_head):
    sem = pltpu.get_barrier_semaphore()
    for off in range(1, n_head):
        peer = seq_id * n_head + lax.rem(head_id + off, n_head)
        pl.semaphore_signal(sem, inc=1, device_id={"cp": peer}, device_id_type=MESH_ID)
    for off in range(1, n_seq):
        peer = lax.rem(seq_id + off, n_seq) * n_head + head_id
        pl.semaphore_signal(sem, inc=1, device_id={"cp": peer}, device_id_type=MESH_ID)
    pl.semaphore_wait(sem, n_head + n_seq - 2)


def remote(src, dst, send, recv, peer):
    return pltpu.make_async_remote_copy(src_ref=src, dst_ref=dst, send_sem=send, recv_sem=recv,
                                        device_id={"cp": peer}, device_id_type=MESH_ID)


def proj_kernel(n_seq, n_head, x_ref, dy_ref, wq, wk, wv, wo, q_out, do_out, k_out, v_out,
                wbuf, obuf, q_st, do_st, k_st, v_st, w_sem, o_sem,
                q_send, q_recv, do_send, do_recv, k_send, k_recv, v_send, v_recv,
                ky_send, ky_recv, vy_send, vy_recv, loc_sem):
    me = lax.axis_index("cp")
    head_id = lax.rem(me, n_head)
    seq_id = lax.div(me, n_head)
    width = q_st.shape[2]
    per_tile = width // HEAD_DIM
    n_kv = n_head // per_tile
    n_pre = N_SLOT - 1

    def dest(step):
        return lax.rem(head_id + 1 + step, n_head)

    def col_tile(tile):
        slot = tile % N_SLOT
        if tile < n_kv:
            src = wk.at[:, pl.ds(tile * width, width)]
        elif tile < 2 * n_kv:
            src = wv.at[:, pl.ds((tile - n_kv) * width, width)]
        else:
            src = wq.at[:, aligned(dest(tile - 2 * n_kv) * width, width)]
        return pltpu.make_async_copy(src, wbuf.at[slot], w_sem.at[slot])

    def q_tile(step):
        slot = lax.rem(step + 2 * n_kv, N_SLOT)
        return pltpu.make_async_copy(wq.at[:, aligned(dest(step) * width, width)], wbuf.at[slot], w_sem.at[slot])

    def o_tile(step):
        slot = lax.rem(step, N_SLOT)
        return pltpu.make_async_copy(wo.at[aligned(dest(step) * width, width), :], obuf.at[slot], o_sem.at[slot])

    for tile in range(n_pre):
        col_tile(tile).start()
    entry_barrier(seq_id, head_id, n_seq, n_head)

    def kv_send(tile):
        stage, out, send, recv, loc = (k_st, k_out, k_send, k_recv, 0) if tile < n_kv else (v_st, v_out, v_send, v_recv, 1)
        for sub in range(per_tile):
            head = (tile % n_kv) * per_tile + sub

            @pl.when(head != head_id)
            def _():
                remote(stage.at[head], out.at[me], send.at[head], recv.at[head_id], seq_id * n_head + head).start()

            @pl.when(head == head_id)
            def _():
                pltpu.make_async_copy(stage.at[head], out.at[me], loc_sem.at[loc]).start()

    for tile in range(2 * n_kv):
        col_tile(tile).wait()
        if tile >= 1:
            kv_send(tile - 1)
        col_tile(tile + n_pre).start()
        prod = mm(x_ref[...], wbuf[tile % N_SLOT]).astype(BF)
        stage = k_st if tile < n_kv else v_st
        for sub in range(per_tile):
            stage[(tile % n_kv) * per_tile + sub] = prod[:, sub * HEAD_DIM:(sub + 1) * HEAD_DIM]

    def send_piece(stage, out, send, recv, loc, step):
        head = dest(step)

        @pl.when(step < n_head - 1)
        def _():
            remote(stage.at[head], out.at[head_id], send.at[head], recv.at[head_id], seq_id * n_head + head).start()

        @pl.when(step == n_head - 1)
        def _():
            pltpu.make_async_copy(stage.at[head], out.at[head_id], loc_sem.at[loc]).start()

    def row_copy(stage, out, send, recv, off, dst_base):
        src = lax.rem(head_id + off, n_head)
        return remote(stage.at[src], out.at[dst_base + src], send.at[src], recv.at[src], seq_id * n_head + src)

    def relay_copy(out, send, recv, off):
        rows = pl.ds(seq_id * n_head, n_head)
        peer = lax.rem(seq_id + off, n_seq) * n_head + head_id
        return remote(out.at[rows], out.at[rows], send.at[off - 1], recv.at[off - 1], peer)

    relay_step = n_head // 2

    def q_step(step, carry):
        q_tile(step).wait()

        @pl.when(step == 0)
        def _():
            kv_send(2 * n_kv - 1)

        @pl.when(step > 0)
        def _():
            send_piece(q_st, q_out, q_send, q_recv, 2, step - 1)

        @pl.when(step + n_pre < n_head)
        def _():
            q_tile(step + n_pre).start()

        @pl.when(step + n_pre >= n_head)
        def _():
            o_tile(step + n_pre - n_head).start()

        @pl.when(step == relay_step)
        def _():
            for stage, out, send, recv, loc in ((k_st, k_out, k_send, k_recv, 0), (v_st, v_out, v_send, v_recv, 1)):
                for off in range(1, n_head):
                    row_copy(stage, out, send, recv, off, seq_id * n_head).wait_recv()
                pltpu.make_async_copy(stage.at[head_id], out.at[me], loc_sem.at[loc]).wait()
            for off in range(1, n_seq):
                relay_copy(k_out, ky_send, ky_recv, off).start()
                relay_copy(v_out, vy_send, vy_recv, off).start()

        slot = lax.rem(step + 2 * n_kv, N_SLOT)
        q_st[dest(step)] = mm(x_ref[...], wbuf[slot]).astype(BF)
        return carry

    lax.fori_loop(0, n_head, q_step, 0)

    def do_step(step, carry):
        o_tile(step).wait()

        @pl.when(step == 0)
        def _():
            send_piece(q_st, q_out, q_send, q_recv, 2, n_head - 1)

        @pl.when(step > 0)
        def _():
            send_piece(do_st, do_out, do_send, do_recv, 3, step - 1)

        @pl.when(step + n_pre < n_head)
        def _():
            o_tile(step + n_pre).start()

        do_st[dest(step)] = mm(dy_ref[...], obuf[lax.rem(step, N_SLOT)], NT).astype(BF)
        return carry

    lax.fori_loop(0, n_head, do_step, 0)
    for off in range(1, n_head):
        row_copy(q_st, q_out, q_send, q_recv, off, 0).wait_recv()
    pltpu.make_async_copy(q_st.at[head_id], q_out.at[head_id], loc_sem.at[2]).wait()
    send_piece(do_st, do_out, do_send, do_recv, 3, n_head - 1)
    for off in range(1, n_head):
        row_copy(k_st, k_out, k_send, k_recv, off, seq_id * n_head).wait_send()
        row_copy(v_st, v_out, v_send, v_recv, off, seq_id * n_head).wait_send()
        row_copy(q_st, q_out, q_send, q_recv, off, 0).wait_send()
        row_copy(do_st, do_out, do_send, do_recv, off, 0).wait()
    for off in range(1, n_seq):
        for out, send, recv in ((k_out, ky_send, ky_recv), (v_out, vy_send, vy_recv)):
            relay_copy(out, send, recv, off).wait_send()
            rows = pl.ds(lax.rem(seq_id + n_seq - off, n_seq) * n_head, n_head)
            remote(out.at[rows], out.at[rows], send.at[off - 1], recv.at[off - 1], me).wait_recv()
    pltpu.make_async_copy(do_st.at[head_id], do_out.at[head_id], loc_sem.at[3]).wait()


def attend_kernel(q_ref, do_ref, k_ref, v_ref, o_ref, dq_ref, dk_ref, dv_ref, kt, vt, s_buf, p_buf):
    n_keys = k_ref.shape[0]
    rows = q_ref.shape[0] * q_ref.shape[1]
    blk = min(UC_ROWS, n_keys)
    n_blk = n_keys // blk
    scale = HEAD_DIM ** -0.5
    gain = scale * LOG2E

    @pl.when((pl.program_id(0) == 0) & (pl.program_id(1) == 0))
    def _():
        def prep(i, carry):
            part = aligned(i * blk, blk)
            kt[:, part] = k_ref[part, :].astype(F32).T.astype(BF)
            vt[:, part] = v_ref[part, :].astype(F32).T.astype(BF)
            dk_ref[part, :] = jnp.zeros((blk, HEAD_DIM), F32)
            dv_ref[part, :] = jnp.zeros((blk, HEAD_DIM), F32)
            return carry
        lax.fori_loop(0, n_blk, prep, 0)

    q_blk = q_ref[...].reshape(rows, HEAD_DIM)
    do_blk = do_ref[...].reshape(rows, HEAD_DIM)

    def score(i, top):
        part = aligned(i * blk, blk)
        s = mm(k_ref[part, :], q_blk, NT)
        s_buf[part, :] = s
        return jnp.maximum(top, jnp.max(s.reshape(blk // 8, 8, rows), axis=0))

    top = lax.fori_loop(0, n_blk, score, jnp.full((8, rows), -jnp.inf, F32))
    top = jnp.max(top, axis=0, keepdims=True)

    def expo(i, tot):
        part = aligned(i * blk, blk)
        e = jnp.exp2((s_buf[part, :] - top) * gain)
        s_buf[part, :] = e
        return tot + jnp.sum(e.reshape(blk // 8, 8, rows), axis=0)

    tot = lax.fori_loop(0, n_blk, expo, jnp.zeros((8, rows), F32))
    inv = 1.0 / jnp.sum(tot, axis=0, keepdims=True)

    def value(i, acc):
        part = aligned(i * blk, blk)
        p = (s_buf[part, :] * inv).astype(BF)
        p_buf[part, :] = p
        return acc + mm(vt[:, part], p)

    out_t = lax.fori_loop(0, n_blk, value, jnp.zeros((HEAD_DIM, rows), F32)).astype(BF).astype(F32)
    o_ref[...] = out_t.T.astype(BF).reshape(o_ref.shape)
    delta = jnp.sum(do_blk.astype(F32).T * out_t, axis=0, keepdims=True)

    def grad(i, acc):
        part = aligned(i * blk, blk)
        p = p_buf[part, :]
        dp = mm(v_ref[part, :], do_blk, NT)
        ds = (p.astype(F32) * (dp - delta)).astype(BF)
        dv_ref[part, :] += mm(p, do_blk)
        dk_ref[part, :] += mm(ds, q_blk)
        return acc + mm(kt[:, part], ds)

    dq_t = lax.fori_loop(0, n_blk, grad, jnp.zeros((HEAD_DIM, rows), F32)) * scale
    dq_ref[...] = dq_t.T.astype(BF).reshape(dq_ref.shape)


def out_kernel(n_seq, n_head, o_in, dq_in, dk_in, dv_in, wq, wk, wv, wo, y_ref, dx_ref,
               wbuf, rbuf, wk_buf, wv_buf, o_full, dq_full, acc, own_k, own_v, rx_k, rx_v, k_st, v_st, dk_full, dv_full,
               w_sem, r_sem, kv_sem, o_send, o_recv, dq_send, dq_recv, yk_send, yk_recv, yv_send, yv_recv,
               k_send, k_recv, v_send, v_recv, loc_sem):
    me = lax.axis_index("cp")
    head_id = lax.rem(me, n_head)
    seq_id = lax.div(me, n_head)
    n_rows = y_ref.shape[0]
    width = o_in.shape[2]
    tile = wbuf.shape[2]
    n_tile = y_ref.shape[1] // tile
    n_pre = N_SLOT - 1

    def col_tile(step):
        slot = lax.rem(step, N_SLOT)
        return pltpu.make_async_copy(wo.at[:, aligned(step * tile, tile)], wbuf.at[slot], w_sem.at[slot])

    def row_tile(step):
        slot = lax.rem(step, N_SLOT)
        return pltpu.make_async_copy(wq.at[aligned(step * tile, tile), :], rbuf.at[slot], r_sem.at[slot])

    wide = aligned(head_id * width, width)
    slim = aligned(head_id * HEAD_DIM, HEAD_DIM)
    local_copies = (
        pltpu.make_async_copy(o_in.at[head_id], o_full.at[:, wide], loc_sem.at[0]),
        pltpu.make_async_copy(dq_in.at[head_id], dq_full.at[:, wide], loc_sem.at[1]),
        pltpu.make_async_copy(dk_in.at[seq_id], own_k, loc_sem.at[2]),
        pltpu.make_async_copy(dv_in.at[seq_id], own_v, loc_sem.at[3]),
    )
    for copy in local_copies:
        copy.start()
    for step in range(n_pre):
        col_tile(step).start()
    entry_barrier(seq_id, head_id, n_seq, n_head)

    def seq_copy(src, rx, send, recv, off):
        peer_seq = lax.rem(seq_id + off, n_seq)
        return remote(src.at[peer_seq], rx.at[off - 1], send.at[off - 1], recv.at[off - 1], peer_seq * n_head + head_id)

    def row_copy(src, dst, cols, send, recv, off):
        head = lax.rem(head_id + off, n_head)
        return remote(src.at[head], dst.at[:, cols], send.at[off - 1], recv.at[off - 1], seq_id * n_head + head)

    for off in range(1, n_seq):
        seq_copy(dk_in, rx_k, yk_send, yk_recv, off).start()
    for off in range(1, n_seq):
        seq_copy(dv_in, rx_v, yv_send, yv_recv, off).start()
    for off in range(1, n_head):
        row_copy(o_in, o_full, wide, o_send, o_recv, off).start()
    for off in range(1, n_head):
        row_copy(dq_in, dq_full, wide, dq_send, dq_recv, off).start()

    def arrived(src, dst, size, send, recv, off):
        head = lax.rem(head_id + n_head - off, n_head)
        remote(src.at[head], dst.at[:, aligned(head * size, size)], send.at[off - 1], recv.at[off - 1], me).wait_recv()

    for off in range(1, n_head):
        arrived(o_in, o_full, width, o_send, o_recv, off)
    local_copies[0].wait()

    def y_step(step, carry):
        col_tile(step).wait()

        @pl.when(step + n_pre < n_tile)
        def _():
            col_tile(step + n_pre).start()

        @pl.when(step + n_pre >= n_tile)
        def _():
            row_tile(step + n_pre - n_tile).start()

        y_ref[:, aligned(step * tile, tile)] = mm(o_full[...], wbuf[lax.rem(step, N_SLOT)]).astype(BF)
        return carry

    lax.fori_loop(0, n_tile, y_step, 0)
    for off in range(1, n_head):
        arrived(dq_in, dq_full, width, dq_send, dq_recv, off)
    local_copies[1].wait()
    kv_copies = (pltpu.make_async_copy(wk, wk_buf, kv_sem.at[0]), pltpu.make_async_copy(wv, wv_buf, kv_sem.at[1]))

    def dx_step(step, carry):
        row_tile(step).wait()

        @pl.when(step + n_pre < n_tile)
        def _():
            row_tile(step + n_pre).start()

        @pl.when(step + n_pre == n_tile)
        def _():
            kv_copies[0].start()
            kv_copies[1].start()

        acc[:, aligned(step * tile, tile)] = mm(dq_full[...], rbuf[lax.rem(step, N_SLOT)], NT)
        return carry

    lax.fori_loop(0, n_tile, dx_step, 0)
    scale = HEAD_DIM ** -0.5

    def reduce_own(src, own, rx, stage, send, recv, copy, gain):
        copy.wait()
        for off in range(1, n_seq):
            remote(src.at[seq_id], rx.at[off - 1], send.at[off - 1], recv.at[off - 1], me).wait_recv()

        def one(head, carry):
            rows = aligned(head * n_rows, n_rows)
            total = own[rows, :]
            for off in range(1, n_seq):
                total = total + rx[off - 1, rows, :]
            stage[head] = (total * gain).astype(BF)
            return carry

        lax.fori_loop(0, n_head, one, 0)

    reduce_own(dk_in, own_k, rx_k, k_st, yk_send, yk_recv, local_copies[2], scale)
    reduce_own(dv_in, own_v, rx_v, v_st, yv_send, yv_recv, local_copies[3], 1.0)
    for off in range(1, n_head):
        row_copy(k_st, dk_full, slim, k_send, k_recv, off).start()
    for off in range(1, n_head):
        row_copy(v_st, dv_full, slim, v_send, v_recv, off).start()
    dk_full[:, slim] = k_st[head_id]
    dv_full[:, slim] = v_st[head_id]
    for copy in kv_copies:
        copy.wait()
    for off in range(1, n_head):
        arrived(k_st, dk_full, HEAD_DIM, k_send, k_recv, off)
    for off in range(1, n_head):
        arrived(v_st, dv_full, HEAD_DIM, v_send, v_recv, off)

    def last_step(step, carry):
        part = aligned(step * tile, tile)
        total = acc[:, part] + mm(dk_full[...], wk_buf[part, :], NT) + mm(dv_full[...], wv_buf[part, :], NT)
        dx_ref[:, part] = total.astype(BF)
        return carry

    lax.fori_loop(0, n_tile, last_step, 0)
    for off in range(1, n_seq):
        seq_copy(dk_in, rx_k, yk_send, yk_recv, off).wait_send()
        seq_copy(dv_in, rx_v, yv_send, yv_recv, off).wait_send()
    for off in range(1, n_head):
        row_copy(o_in, o_full, wide, o_send, o_recv, off).wait_send()
        row_copy(dq_in, dq_full, wide, dq_send, dq_recv, off).wait_send()
        row_copy(k_st, dk_full, slim, k_send, k_recv, off).wait_send()
        row_copy(v_st, dv_full, slim, v_send, v_recv, off).wait_send()


def solution(mesh):
    n_group = mesh.shape["cp"]
    row_spec = P(("dp", "cp"), None)
    full_spec = P(None, None)
    any_spec = pl.BlockSpec(memory_space=pl.ANY)
    vmem_spec = pl.BlockSpec(memory_space=pltpu.VMEM)
    dma = pltpu.SemaphoreType.DMA

    def local_body(x_loc, dy_loc, w_q, w_k, w_v, w_o):
        n_rows, n_model = x_loc.shape
        n_head = w_k.shape[1] // HEAD_DIM
        width = w_q.shape[1] // n_head
        q_group = width // HEAD_DIM
        n_seq = n_group // n_head
        n_keys = n_rows * n_group
        tile = width

        q_all, do_all, k_all, v_all = pl.pallas_call(
            functools.partial(proj_kernel, n_seq, n_head),
            out_shape=(jax.ShapeDtypeStruct((n_head, n_rows, width), BF), jax.ShapeDtypeStruct((n_head, n_rows, width), BF),
                       jax.ShapeDtypeStruct((n_group, n_rows, HEAD_DIM), BF), jax.ShapeDtypeStruct((n_group, n_rows, HEAD_DIM), BF)),
            in_specs=[vmem_spec, vmem_spec] + [any_spec] * 4,
            out_specs=(any_spec,) * 4,
            scratch_shapes=[pltpu.VMEM((N_SLOT, n_model, width), BF), pltpu.VMEM((N_SLOT, width, n_model), BF),
                            pltpu.VMEM((n_head, n_rows, width), BF), pltpu.VMEM((n_head, n_rows, width), BF),
                            pltpu.VMEM((n_head, n_rows, HEAD_DIM), BF), pltpu.VMEM((n_head, n_rows, HEAD_DIM), BF),
                            dma((N_SLOT,)), dma((N_SLOT,))]
                           + [dma((n_head,))] * 8 + [dma((n_seq - 1,))] * 4 + [dma((4,))],
            compiler_params=pltpu.CompilerParams(collective_id=0, has_side_effects=True, vmem_limit_bytes=VMEM_BYTES),
            name="proj_scatter",
        )(x_loc, dy_loc, w_q, w_k, w_v, w_o)

        n_src = max(1, min(n_head, BQ_ROWS // n_rows))
        rows = n_src * n_rows
        blk_spec = pl.BlockSpec((n_src, n_rows, HEAD_DIM), lambda j, b: (b, 0, j))
        key_spec = pl.BlockSpec((n_keys, HEAD_DIM), lambda j, b: (0, 0))
        o_blk, dq_blk, dk_part, dv_part = pl.pallas_call(
            attend_kernel,
            grid=(q_group, n_head // n_src),
            out_shape=(jax.ShapeDtypeStruct((n_head, n_rows, width), BF), jax.ShapeDtypeStruct((n_head, n_rows, width), BF),
                       jax.ShapeDtypeStruct((n_keys, HEAD_DIM), F32), jax.ShapeDtypeStruct((n_keys, HEAD_DIM), F32)),
            in_specs=[blk_spec, blk_spec, key_spec, key_spec],
            out_specs=(blk_spec, blk_spec, key_spec, key_spec),
            scratch_shapes=[pltpu.VMEM((HEAD_DIM, n_keys), BF), pltpu.VMEM((HEAD_DIM, n_keys), BF),
                            pltpu.VMEM((n_keys, rows), F32), pltpu.VMEM((n_keys, rows), BF)],
            compiler_params=pltpu.CompilerParams(dimension_semantics=("arbitrary", "arbitrary"), vmem_limit_bytes=VMEM_BYTES),
            name="attend",
        )(q_all, do_all, k_all.reshape(n_keys, HEAD_DIM), v_all.reshape(n_keys, HEAD_DIM))

        seq_rows = n_head * n_rows
        part_shape = (n_seq, seq_rows, HEAD_DIM)
        y_loc, dx_loc = pl.pallas_call(
            functools.partial(out_kernel, n_seq, n_head),
            out_shape=(jax.ShapeDtypeStruct((n_rows, n_model), BF), jax.ShapeDtypeStruct((n_rows, n_model), BF)),
            in_specs=[any_spec] * 8,
            out_specs=(vmem_spec, vmem_spec),
            scratch_shapes=[pltpu.VMEM((N_SLOT, w_o.shape[0], tile), BF), pltpu.VMEM((N_SLOT, tile, w_q.shape[1]), BF),
                            pltpu.VMEM(w_k.shape, BF), pltpu.VMEM(w_v.shape, BF),
                            pltpu.VMEM((n_rows, w_q.shape[1]), BF), pltpu.VMEM((n_rows, w_q.shape[1]), BF),
                            pltpu.VMEM((n_rows, n_model), F32),
                            pltpu.VMEM((seq_rows, HEAD_DIM), F32), pltpu.VMEM((seq_rows, HEAD_DIM), F32),
                            pltpu.VMEM((n_seq - 1, seq_rows, HEAD_DIM), F32), pltpu.VMEM((n_seq - 1, seq_rows, HEAD_DIM), F32),
                            pltpu.VMEM((n_head, n_rows, HEAD_DIM), BF), pltpu.VMEM((n_head, n_rows, HEAD_DIM), BF),
                            pltpu.VMEM((n_rows, w_k.shape[1]), BF), pltpu.VMEM((n_rows, w_v.shape[1]), BF),
                            dma((N_SLOT,)), dma((N_SLOT,)), dma((2,))]
                           + [dma((n_head - 1,))] * 4 + [dma((n_seq - 1,))] * 4 + [dma((n_head - 1,))] * 4 + [dma((4,))],
            compiler_params=pltpu.CompilerParams(collective_id=1, has_side_effects=True, vmem_limit_bytes=VMEM_BYTES),
            name="gather_out",
        )(o_blk, dq_blk, dk_part.reshape(part_shape), dv_part.reshape(part_shape), w_q, w_k, w_v, w_o)
        return y_loc, dx_loc

    return jax.shard_map(local_body, mesh=mesh,
                         in_specs=(row_spec, row_spec, full_spec, full_spec, full_spec, full_spec),
                         out_specs=(row_spec, row_spec), check_vma=False)
```

time: 618 us -> 212 us (0.34); the launches traced: 610 us -> 212 us
  matrix products: 311 us -> 0 us
  waiting for transfers between devices: 234 us -> 0 us
  Pallas kernels: 0 us -> 206 us
  other arithmetic: 34.5 us -> 0 us
  between operations: 14.4 us -> 0.65 us
  local copies, waits for them, and re-layouts: 15.1 us -> 4.57 us
    dot_general x22 -> x0, matrix products: 311 us -> none  [the longest x4 57.6 us: one_block(): jnp.einsum('thjd,uhd->thju', q_blk, k_all, preferred_element_type=jnp.flo...]
    pallas_call x0 -> x3, Pallas kernels: none -> 206 us  [the longest x1 96.6 us: local_body(): pl.pallas_call(attend_kernel, grid=(q_group, n_head // n_src), out_shape=...]
    reduce_scatter x2 -> x0, waiting for transfers between devices: 172 us -> none  [the longest x1 102 us: local_body(): lax.psum_scatter(dv_part, 'cp', scatter_dimension=0, tiled=True)]
    all_gather x2 -> x0, waiting for transfers between devices: 60.6 us -> none  [the longest x1 49 us: local_body(): v_all = lax.all_gather(v_loc, 'cp', axis=0, tiled=True)]
    reduce_sum x2 -> x0, other arithmetic: 28.1 us -> none  [one_block(): lse_blk = jax.nn.logsumexp(scores, axis=-1, keepdims=True)]
  transfers between devices with their start and end apart: 4 -> 0, of which waited for: 4 -> 0; matrix products, arithmetic and copies ran while one was open for 13% -> 0% of each run, Pallas kernels for 0% -> 0%
where the time goes in v1:
time: 212 us
  Pallas kernels  206 us (97%)
  local copies, waits for them, and re-layouts  4.57 us (2%)
    pallas_call x1, Pallas kernels, local_body(): pl.pallas_call(attend_kernel, grid=(q_group, n_head // n_src), out_shape=...  96.6 us
    pallas_call x1, Pallas kernels, local_body(): pl.pallas_call(functools.partial(out_kernel, n_seq, n_head), out_shape=(j...  65.5 us
    pallas_call x1, Pallas kernels, local_body(): pl.pallas_call(functools.partial(proj_kernel, n_seq, n_head), out_shape=(...  44.3 us
    unnamed x2, local copies, waits for them, and re-layouts  4.57 us

profile of v1, /device:TPU:97, one launch (start us, length us, event | category | flops | bytes accessed | tf_op | source)
XLA Modules:
  0.0 211.5 jit_solution(13371990579412325940)
XLA Ops:
  0.6 44.3 %proj_scatter.1 = (bf16[8,128,512]{2,1,0:T(8,128)(2,1)}, bf16[8,128,512]{2,1,0:T(8,128)(2,1)}, bf16[32,128,128]{2,1,0:T(8,128)(2,1)}, bf16[32,128,128]{2,1,0:T(8,128)(2,1)}) custom-call(bf16[128,4096]{1,0:T(8,128)(2,1)} %x_ref.1, bf16[128,4096]{1,0:T(8,128)(2,1)} %dy_ref.1, bf16[4096,4096]{1,0:T(8,128)(2,1)} %wq.3, bf16[4096,1024]{1,0:T(8,128)(2,1)} %wk.3, ...), custom_call_target="tpu_custom_call" | custom-call | tf_op jit(solution)/shard_map/proj_scatter/pallas_call | solution.py:425
  44.9 96.6 %attend.1 = (bf16[8,128,512]{2,1,0:T(8,128)(2,1)}, bf16[8,128,512]{2,1,0:T(8,128)(2,1)}, f32[4096,128]{1,0:T(8,128)}, f32[4096,128]{1,0:T(8,128)}) custom-call(bf16[8,128,512]{2,1,0:T(8,128)(2,1)} %get-tuple-element.10.q_ref, bf16[8,128,512]{2,1,0:T(8,128)(2,1)} %get-tuple-element.11.do_ref, bf16[4096,128]{1,0:T(8,128)(2,1)} %bitcast.6, ...), custom_call_target="tpu_custom_call" | custom-call | tf_op jit(solution)/shard_map/attend/pallas_call | solution.py:444
  141.5 65.5 %gather_out.1 = (bf16[128,4096]{1,0:T(8,128)(2,1)}, bf16[128,4096]{1,0:T(8,128)(2,1)}) custom-call(bf16[8,128,512]{2,1,0:T(8,128)(2,1)} %get-tuple-element.14.o_in, bf16[8,128,512]{2,1,0:T(8,128)(2,1)} %get-tuple-element.15.dq_in, f32[4,1024,128]{2,1,0:T(8,128)} %bitcast.4, f32[4,1024,128]{2,1,0:T(8,128)} %bitcast.5, bf16[4096,4096]{1,0:T(8,128)(2,1)} %wq.3, ...), custom_call_target="tpu_custom_call" | custom-call | tf_op jit(solution)/shard_map/gather_out/pallas_call | solution.py:459
  207.0 2.3 %copy.10 = bf16[128,4096]{1,0:T(8,128)(2,1)} copy(bf16[128,4096]{1,0:T(8,128)(2,1)} %get-tuple-element.20) | data formatting | bytes 2097152
  209.3 2.3 %copy.11 = bf16[128,4096]{1,0:T(8,128)(2,1)} copy(bf16[128,4096]{1,0:T(8,128)(2,1)} %get-tuple-element.21) | data formatting | bytes 2097152

commit v2 on v1

v2 whole, which is shorter than its diff:
```python
import functools

import jax
import jax.numpy as jnp
from jax import lax
from jax.experimental import pallas as pl
from jax.experimental.pallas import tpu as pltpu
from jax.sharding import PartitionSpec as P

HEAD_DIM = 128
LOG2E = 1.4426950408889634
N_SLOT = 4
BQ_ROWS = 512
UC_ROWS = 512
VMEM_BYTES = 62 * 1024 * 1024
VMEM_MAIN = 67000000
MESH_ID = pl.DeviceIdType.MESH
BF = jnp.bfloat16
F32 = jnp.float32
NT = (((1,), (1,)), ((), ()))
NN = (((1,), (0,)), ((), ()))


def mm(a, b, dims=NN):
    return lax.dot_general(a, b, dims, preferred_element_type=F32)


def aligned(start, size):
    return pl.ds(pl.multiple_of(start, size), size)


def entry_barrier(seq_id, head_id, n_seq, n_head):
    sem = pltpu.get_barrier_semaphore()
    for off in range(1, n_head):
        peer = seq_id * n_head + lax.rem(head_id + off, n_head)
        pl.semaphore_signal(sem, inc=1, device_id={"cp": peer}, device_id_type=MESH_ID)
    for off in range(1, n_seq):
        peer = lax.rem(seq_id + off, n_seq) * n_head + head_id
        pl.semaphore_signal(sem, inc=1, device_id={"cp": peer}, device_id_type=MESH_ID)
    pl.semaphore_wait(sem, n_head + n_seq - 2)


def remote(src, dst, send, recv, peer):
    return pltpu.make_async_remote_copy(src_ref=src, dst_ref=dst, send_sem=send, recv_sem=recv,
                                        device_id={"cp": peer}, device_id_type=MESH_ID)


def proj_kernel(n_seq, n_head, x_ref, dy_ref, wq, wk, wv, wo, q_out, do_out, k_out, v_out,
                wbuf, obuf, q_st, k_st, v_st, w_sem, o_sem,
                q_send, q_recv, k_send, k_recv, v_send, v_recv,
                ky_send, ky_recv, vy_send, vy_recv, loc_sem):
    me = lax.axis_index("cp")
    head_id = lax.rem(me, n_head)
    seq_id = lax.div(me, n_head)
    width = q_st.shape[2]
    per_tile = width // HEAD_DIM
    n_kv = n_head // per_tile
    n_pre = N_SLOT - 1

    def dest(step):
        return lax.rem(head_id + 1 + step, n_head)

    def col_tile(tile):
        slot = tile % N_SLOT
        if tile < n_kv:
            src = wk.at[:, pl.ds(tile * width, width)]
        elif tile < 2 * n_kv:
            src = wv.at[:, pl.ds((tile - n_kv) * width, width)]
        else:
            src = wq.at[:, aligned(dest(tile - 2 * n_kv) * width, width)]
        return pltpu.make_async_copy(src, wbuf.at[slot], w_sem.at[slot])

    def q_tile(step):
        slot = lax.rem(step + 2 * n_kv, N_SLOT)
        return pltpu.make_async_copy(wq.at[:, aligned(dest(step) * width, width)], wbuf.at[slot], w_sem.at[slot])

    def o_tile(step):
        slot = lax.rem(step, N_SLOT)
        return pltpu.make_async_copy(wo.at[aligned(dest(step) * width, width), :], obuf.at[slot], o_sem.at[slot])

    for tile in range(n_pre):
        col_tile(tile).start()
    entry_barrier(seq_id, head_id, n_seq, n_head)

    def kv_send(tile):
        stage, out, send, recv, loc = (k_st, k_out, k_send, k_recv, 0) if tile < n_kv else (v_st, v_out, v_send, v_recv, 1)
        for sub in range(per_tile):
            head = (tile % n_kv) * per_tile + sub

            @pl.when(head != head_id)
            def _():
                remote(stage.at[head], out.at[me], send.at[head], recv.at[head_id], seq_id * n_head + head).start()

            @pl.when(head == head_id)
            def _():
                pltpu.make_async_copy(stage.at[head], out.at[me], loc_sem.at[loc]).start()

    for tile in range(2 * n_kv):
        col_tile(tile).wait()
        if tile >= 1:
            kv_send(tile - 1)
        col_tile(tile + n_pre).start()
        prod = mm(x_ref[...], wbuf[tile % N_SLOT]).astype(BF)
        stage = k_st if tile < n_kv else v_st
        for sub in range(per_tile):
            stage[(tile % n_kv) * per_tile + sub] = prod[:, sub * HEAD_DIM:(sub + 1) * HEAD_DIM]

    def send_piece(stage, out, send, recv, loc, step):
        head = dest(step)

        @pl.when(step < n_head - 1)
        def _():
            remote(stage.at[head], out.at[head_id], send.at[head], recv.at[head_id], seq_id * n_head + head).start()

        @pl.when(step == n_head - 1)
        def _():
            pltpu.make_async_copy(stage.at[head], out.at[head_id], loc_sem.at[loc]).start()

    def row_copy(stage, out, send, recv, off, dst_base):
        src = lax.rem(head_id + off, n_head)
        return remote(stage.at[src], out.at[dst_base + src], send.at[src], recv.at[src], seq_id * n_head + src)

    ahead, behind = 1, n_seq - 1

    def seq_copy(out, send, recv, slot, origin, off):
        rows = pl.ds(lax.rem(seq_id + origin, n_seq) * n_head, n_head)
        peer = lax.rem(seq_id + off, n_seq) * n_head + head_id
        return remote(out.at[rows], out.at[rows], send.at[slot], recv.at[slot], peer)

    relays = ((k_out, ky_send, ky_recv, ahead), (v_out, vy_send, vy_recv, behind))

    def forward():
        for out, send, recv, off in relays:
            seq_copy(out, send, recv, 0, n_seq - off, off).wait_recv()
            seq_copy(out, send, recv, 2, n_seq - off, off).start()

    relay_step = n_head // 2

    def q_step(step, carry):
        q_tile(step).wait()

        @pl.when(step == 0)
        def _():
            kv_send(2 * n_kv - 1)

        @pl.when(step > 0)
        def _():
            send_piece(q_st, q_out, q_send, q_recv, 2, step - 1)

        @pl.when(step + n_pre < n_head)
        def _():
            q_tile(step + n_pre).start()

        @pl.when(step + n_pre >= n_head)
        def _():
            o_tile(step + n_pre - n_head).start()

        @pl.when(step == relay_step)
        def _():
            for stage, out, send, recv, loc in ((k_st, k_out, k_send, k_recv, 0), (v_st, v_out, v_send, v_recv, 1)):
                for off in range(1, n_head):
                    row_copy(stage, out, send, recv, off, seq_id * n_head).wait_recv()
                pltpu.make_async_copy(stage.at[head_id], out.at[me], loc_sem.at[loc]).wait()
            for out, send, recv, off in relays:
                seq_copy(out, send, recv, 0, 0, off).start()
                seq_copy(out, send, recv, 1, 0, n_seq - off).start()

        slot = lax.rem(step + 2 * n_kv, N_SLOT)
        q_st[dest(step)] = mm(x_ref[...], wbuf[slot]).astype(BF)
        return carry

    lax.fori_loop(0, n_head, q_step, 0)

    forward_step = (5 * n_head) // 8

    def do_step(step, carry):
        o_tile(step).wait()

        @pl.when(step == 0)
        def _():
            send_piece(q_st, q_out, q_send, q_recv, 2, n_head - 1)

        @pl.when(step == forward_step)
        def _():
            forward()

        @pl.when(step + n_pre < n_head)
        def _():
            o_tile(step + n_pre).start()

        do_out[dest(step)] = mm(dy_ref[...], obuf[lax.rem(step, N_SLOT)], NT).astype(BF)
        return carry

    lax.fori_loop(0, n_head, do_step, 0)
    for off in range(1, n_head):
        row_copy(q_st, q_out, q_send, q_recv, off, 0).wait()
        row_copy(k_st, k_out, k_send, k_recv, off, seq_id * n_head).wait_send()
        row_copy(v_st, v_out, v_send, v_recv, off, seq_id * n_head).wait_send()
    pltpu.make_async_copy(q_st.at[head_id], q_out.at[head_id], loc_sem.at[2]).wait()
    for out, send, recv, off in relays:
        seq_copy(out, send, recv, 0, 0, off).wait_send()
        seq_copy(out, send, recv, 1, 0, n_seq - off).wait_send()
        seq_copy(out, send, recv, 2, n_seq - off, off).wait_send()
        seq_copy(out, send, recv, 1, off, off).wait_recv()
        seq_copy(out, send, recv, 2, 2, off).wait_recv()


def main_kernel(n_seq, n_head, q_in, do_in, k_in, v_in, wq, wk, wv, wo, y_ref, dx_ref,
                p_all, s_buf, q_vm, k_vm, v_vm, kt, vt, do_vm, o_vm, dq_vm, o_full, dq_full, delta_ref,
                dk_acc, dv_acc, mid_k, mid_v, rx_k, rx_v, k_st, v_st, dk_full, dv_full,
                in_sem, w_sem, loc_sem, do_send, do_recv, o_send, o_recv, dq_send, dq_recv,
                k_send, k_recv, v_send, v_recv, yk_send, yk_recv, yv_send, yv_recv):
    me = lax.axis_index("cp")
    head_id = lax.rem(me, n_head)
    seq_id = lax.div(me, n_head)
    n_keys = k_vm.shape[0]
    n_rows, width = q_vm.shape[1], q_vm.shape[2]
    q_group = width // HEAD_DIM
    n_step, _, rows = p_all.shape
    n_src = rows // n_rows
    n_blk = n_step // q_group
    tile = p_all.shape[2]
    n_tile = y_ref.shape[1] // tile
    blk = min(UC_ROWS, n_keys // n_seq)
    n_chunk = n_keys // blk
    part_keys = n_keys // n_seq
    scale = HEAD_DIM ** -0.5
    gain = scale * LOG2E
    ahead, behind = 1, n_seq - 1

    def row_peer(off):
        return lax.rem(head_id + off, n_head)

    def row_copy(src, dst, send, recv, off):
        return remote(src.at[row_peer(off)], dst, send.at[off - 1], recv.at[off - 1], seq_id * n_head + row_peer(off))

    def col_copy(src, dst, send, recv, slot, off):
        return remote(src, dst, send.at[slot], recv.at[slot], lax.rem(seq_id + off, n_seq) * n_head + head_id)

    wide = aligned(head_id * width, width)
    slim = aligned(head_id * HEAD_DIM, HEAD_DIM)

    def from_peer(off):
        return row_peer(n_head - off)

    loads = (pltpu.make_async_copy(k_in, k_vm, in_sem.at[0]), pltpu.make_async_copy(q_in, q_vm, in_sem.at[1]),
             pltpu.make_async_copy(v_in, v_vm, in_sem.at[2]),
             pltpu.make_async_copy(do_in.at[head_id], do_vm.at[head_id], in_sem.at[3]))
    for copy in loads:
        copy.start()
    entry_barrier(seq_id, head_id, n_seq, n_head)
    for off in range(1, n_head):
        row_copy(do_in, do_vm.at[head_id], do_send, do_recv, off).start()
    for copy in loads[:3]:
        copy.wait()

    def prep(i, carry):
        part = aligned(i * blk, blk)
        kt[:, part] = k_vm[part, :].astype(F32).T.astype(BF)
        vt[:, part] = v_vm[part, :].astype(F32).T.astype(BF)
        return carry

    lax.fori_loop(0, n_chunk, prep, 0)

    def block_of(step):
        return pl.ds(lax.rem(step, n_blk) * n_src, n_src), aligned(lax.div(step, n_blk) * HEAD_DIM, HEAD_DIM)

    def read_block(ref, step):
        srcs, cols = block_of(step)
        return ref[srcs, :, cols].reshape(rows, HEAD_DIM)

    def forward(step, carry):
        q_blk = read_block(q_vm, step)

        def score(i, top):
            part = aligned(i * blk, blk)
            s = mm(k_vm[part, :], q_blk, NT)
            s_buf[part, :] = s
            return jnp.maximum(top, jnp.max(s.reshape(blk // 8, 8, rows), axis=0))

        top = lax.fori_loop(0, n_chunk, score, jnp.full((8, rows), -jnp.inf, F32))
        top = jnp.max(top, axis=0, keepdims=True)

        def expo(i, tot):
            part = aligned(i * blk, blk)
            e = jnp.exp2((s_buf[part, :] - top) * gain)
            s_buf[part, :] = e
            return tot + jnp.sum(e.reshape(blk // 8, 8, rows), axis=0)

        tot = lax.fori_loop(0, n_chunk, expo, jnp.zeros((8, rows), F32))
        inv = 1.0 / jnp.sum(tot, axis=0, keepdims=True)

        def value(i, acc):
            part = aligned(i * blk, blk)
            p = (s_buf[part, :] * inv).astype(BF)
            p_all[step, part, :] = p
            return acc + mm(vt[:, part], p)

        out_t = lax.fori_loop(0, n_chunk, value, jnp.zeros((HEAD_DIM, rows), F32))
        srcs, cols = block_of(step)
        o_vm[srcs, :, cols] = out_t.T.astype(BF).reshape(n_src, n_rows, HEAD_DIM)
        return carry

    lax.fori_loop(0, n_step, forward, 0)
    loads[3].wait()
    for off in range(1, n_head):
        remote(do_in.at[row_peer(off)], do_vm.at[from_peer(off)], do_send.at[off - 1], do_recv.at[off - 1], me).wait_recv()

    def row_delta(step, carry):
        prod = read_block(do_vm, step).astype(F32) * read_block(o_vm, step).astype(F32)
        delta_ref[step] = jnp.broadcast_to(jnp.sum(prod.T, axis=0, keepdims=True), (8, rows))
        return carry

    lax.fori_loop(0, n_step, row_delta, 0)
    keep_o = pltpu.make_async_copy(o_vm.at[head_id], o_full.at[:, wide], loc_sem.at[0])
    keep_o.start()
    for off in range(1, n_head):
        row_copy(o_vm, o_full.at[:, wide], o_send, o_recv, off).start()

    dq_base = n_tile * n_rows

    def o_tile(step):
        return pltpu.make_async_copy(wo.at[:, aligned(step * tile, tile)], p_all.at[step], w_sem.at[step])

    def grad_steps(order, low, high):
        off = (2, ahead, behind, 0)[order]
        first, last = order == 0, order == n_seq - 1
        base = lax.rem(seq_id + off, n_seq) * part_keys

        def one(step, carry):
            if last:
                @pl.when(step > 0)
                def _():
                    o_tile(step - 1).start()
            q_blk = read_block(q_vm, step)
            do_blk = read_block(do_vm, step)
            delta = delta_ref[step][0:1, :]
            dq_rows = aligned(dq_base + step * HEAD_DIM, HEAD_DIM)
            acc = None if first else s_buf[dq_rows, :]
            for i in range(part_keys // blk):
                part = aligned(base + i * blk, blk)
                here = pl.ds(i * blk, blk)
                p = p_all[step, part, :]
                dp = mm(v_vm[part, :], do_blk, NT)
                ds = (p.astype(F32) * (dp - delta)).astype(BF)
                dv_acc[order, here, :] += mm(p, do_blk)
                dk_acc[order, here, :] += mm(ds, q_blk)
                add = mm(kt[:, part], ds)
                acc = add if acc is None else acc + add
            if last:
                srcs, cols = block_of(step)
                dq_vm[srcs, :, cols] = (acc * scale).T.astype(BF).reshape(n_src, n_rows, HEAD_DIM)
            else:
                s_buf[dq_rows, :] = acc
            return carry

        lax.fori_loop(low, high, one, 0)

    def clear(order):
        dk_acc[order] = jnp.zeros((part_keys, HEAD_DIM), F32)
        dv_acc[order] = jnp.zeros((part_keys, HEAD_DIM), F32)

    def add_into(acc, order, other):
        def one(i, carry):
            part = aligned(i * n_rows, n_rows)
            acc[order, part, :] += other[part, :]
            return carry
        lax.fori_loop(0, part_keys // n_rows, one, 0)

    early = n_step // 4
    sends = (
        (col_copy(dk_acc.at[0], mid_k, yk_send, yk_recv, 0, ahead), col_copy(dv_acc.at[0], mid_v, yv_send, yv_recv, 0, behind)),
        (col_copy(dk_acc.at[1], rx_k.at[0], yk_send, yk_recv, 1, ahead), col_copy(dv_acc.at[1], rx_v.at[1], yv_send, yv_recv, 2, ahead)),
        (col_copy(dv_acc.at[2], rx_v.at[0], yv_send, yv_recv, 1, behind), col_copy(dk_acc.at[2], rx_k.at[1], yk_send, yk_recv, 2, behind)),
    )
    for order in range(n_seq):
        clear(order)
        if order == 1:
            for copy in sends[0]:
                copy.start()
        if order < 2:
            grad_steps(order, 0, n_step)
            continue
        grad_steps(order, 0, early)
        if order == 2:
            sends[0][0].wait_recv()
            add_into(dk_acc, 1, mid_k)
        else:
            sends[0][1].wait_recv()
            add_into(dv_acc, 2, mid_v)
        sends[order - 1][1].start()
        sends[order - 1][0].start()
        grad_steps(order, early, n_step)
    o_tile(n_step - 1).start()
    dq_full[head_id] = dq_vm[head_id]
    for off in range(1, n_head):
        row_copy(dq_vm, dq_full.at[head_id], dq_send, dq_recv, off).start()
    keep_o.wait()
    for off in range(1, n_head):
        remote(o_vm.at[row_peer(off)], o_full.at[:, aligned(from_peer(off) * width, width)],
               o_send.at[off - 1], o_recv.at[off - 1], me).wait_recv()

    def q_tile(step):
        src = lax.rem(head_id + n_head - step, n_head)
        return pltpu.make_async_copy(wq.at[:, aligned(src * width, width)], p_all.at[step], w_sem.at[step])

    def y_step(step, carry):
        o_tile(step).wait()

        @pl.when(step > 0)
        def _():
            q_tile(step - 1).start()

        y_ref[:, aligned(step * tile, tile)] = mm(o_full[...], p_all[step]).astype(BF)
        return carry

    lax.fori_loop(0, n_tile, y_step, 0)
    q_tile(n_tile - 1).start()
    n_kv = wk.shape[1] // tile
    kv_tiles = [pltpu.make_async_copy(src.at[:, pl.ds(t * tile, tile)], p_all.at[which * n_kv + t], w_sem.at[which * n_kv + t])
                for which, src in enumerate((wk, wv)) for t in range(n_kv)]

    def dx_piece(step, first):
        src = lax.rem(head_id + n_head - step, n_head)
        for e in range(n_tile):
            here = pl.ds(e * n_rows, n_rows)
            add = mm(dq_full[src], p_all[step, e * tile:(e + 1) * tile, :], NT)
            s_buf[here, :] = add if first else s_buf[here, :] + add

    def dx_step(step, carry):
        q_tile(step).wait()
        src = lax.rem(head_id + n_head - step, n_head)
        remote(dq_vm.at[src], dq_full.at[src], dq_send.at[step - 1], dq_recv.at[step - 1], me).wait_recv()
        dx_piece(step, False)
        return carry

    q_tile(0).wait()
    dx_piece(0, True)
    half = n_head // 2
    lax.fori_loop(1, half, dx_step, 0)
    for copy in kv_tiles[:half]:
        copy.start()

    def reduce_own(acc, rx, stage, send, recv, gain):
        for slot, off in ((1, ahead), (2, behind)):
            col_copy(acc.at[0], rx.at[slot - 1], send, recv, slot, off).wait_recv()

        def one(head, carry):
            part = aligned(head * n_rows, n_rows)
            stage[head] = ((acc[n_seq - 1, part, :] + rx[0, part, :] + rx[1, part, :]) * gain).astype(BF)
            return carry

        lax.fori_loop(0, n_head, one, 0)

    reduce_own(dk_acc, rx_k, k_st, yk_send, yk_recv, scale)
    reduce_own(dv_acc, rx_v, v_st, yv_send, yv_recv, 1.0)
    for stage, full, send, recv in ((k_st, dk_full, k_send, k_recv), (v_st, dv_full, v_send, v_recv)):
        for off in range(1, n_head):
            row_copy(stage, full.at[:, slim], send, recv, off).start()
        full[:, slim] = stage[head_id]
    lax.fori_loop(half, n_head, dx_step, 0)
    for copy in kv_tiles[half:]:
        copy.start()
    for stage, full, send, recv in ((k_st, dk_full, k_send, k_recv), (v_st, dv_full, v_send, v_recv)):
        for off in range(1, n_head):
            remote(stage.at[row_peer(off)], full.at[:, aligned(from_peer(off) * HEAD_DIM, HEAD_DIM)],
                   send.at[off - 1], recv.at[off - 1], me).wait_recv()
    for copy in kv_tiles:
        copy.wait()

    def last_step(e, carry):
        part = aligned(e * tile, tile)
        total = s_buf[aligned(e * n_rows, n_rows), :]
        for which, full in enumerate((dk_full, dv_full)):
            for t in range(n_kv):
                total = total + mm(full[:, t * tile:(t + 1) * tile], p_all[which * n_kv + t, part, :], NT)
        dx_ref[:, part] = total.astype(BF)
        return carry

    lax.fori_loop(0, n_tile, last_step, 0)
    for group in sends:
        for copy in group:
            copy.wait_send()
    for off in range(1, n_head):
        row_copy(do_in, do_vm.at[head_id], do_send, do_recv, off).wait_send()
        row_copy(o_vm, o_full.at[:, wide], o_send, o_recv, off).wait_send()
        row_copy(dq_vm, dq_full.at[head_id], dq_send, dq_recv, off).wait_send()
        row_copy(k_st, dk_full.at[:, slim], k_send, k_recv, off).wait_send()
        row_copy(v_st, dv_full.at[:, slim], v_send, v_recv, off).wait_send()


def solution(mesh):
    n_group = mesh.shape["cp"]
    row_spec = P(("dp", "cp"), None)
    full_spec = P(None, None)
    any_spec = pl.BlockSpec(memory_space=pl.ANY)
    vmem_spec = pl.BlockSpec(memory_space=pltpu.VMEM)
    dma = pltpu.SemaphoreType.DMA

    def local_body(x_loc, dy_loc, w_q, w_k, w_v, w_o):
        n_rows, n_model = x_loc.shape
        n_head = w_k.shape[1] // HEAD_DIM
        width = w_q.shape[1] // n_head
        q_group = width // HEAD_DIM
        n_seq = n_group // n_head
        n_keys = n_rows * n_group
        piece = jax.ShapeDtypeStruct((n_head, n_rows, width), BF)
        keys = jax.ShapeDtypeStruct((n_group, n_rows, HEAD_DIM), BF)
        q_all, do_own, k_all, v_all = pl.pallas_call(
            functools.partial(proj_kernel, n_seq, n_head),
            out_shape=(piece, piece, keys, keys),
            in_specs=[vmem_spec, vmem_spec] + [any_spec] * 4,
            out_specs=(any_spec, vmem_spec, any_spec, any_spec),
            scratch_shapes=[pltpu.VMEM((N_SLOT, n_model, width), BF), pltpu.VMEM((N_SLOT, width, n_model), BF),
                            pltpu.VMEM((n_head, n_rows, width), BF),
                            pltpu.VMEM((n_head, n_rows, HEAD_DIM), BF), pltpu.VMEM((n_head, n_rows, HEAD_DIM), BF),
                            dma((N_SLOT,)), dma((N_SLOT,))]
                           + [dma((n_head,))] * 6 + [dma((3,))] * 4 + [dma((3,))],
            compiler_params=pltpu.CompilerParams(collective_id=0, has_side_effects=True, vmem_limit_bytes=VMEM_BYTES),
            name="proj_scatter",
        )(x_loc, dy_loc, w_q, w_k, w_v, w_o)

        rows = max(1, min(n_head, BQ_ROWS // n_rows)) * n_rows
        n_step = q_group * n_head * n_rows // rows
        part_keys = n_keys // n_seq
        acts = pltpu.VMEM((n_head, n_rows, width), BF)
        flat = pltpu.VMEM((n_rows, n_head * width), BF)
        head_keys = pltpu.VMEM((n_keys, HEAD_DIM), BF)
        head_keys_t = pltpu.VMEM((HEAD_DIM, n_keys), BF)
        sums = pltpu.VMEM((n_seq, part_keys, HEAD_DIM), F32)
        mid = pltpu.VMEM((part_keys, HEAD_DIM), F32)
        pair = pltpu.VMEM((2, part_keys, HEAD_DIM), F32)
        stage = pltpu.VMEM((n_head, n_rows, HEAD_DIM), BF)
        slim = pltpu.VMEM((n_rows, n_head * HEAD_DIM), BF)
        y_loc, dx_loc = pl.pallas_call(
            functools.partial(main_kernel, n_seq, n_head),
            out_shape=(jax.ShapeDtypeStruct((n_rows, n_model), BF), jax.ShapeDtypeStruct((n_rows, n_model), BF)),
            in_specs=[any_spec] * 8,
            out_specs=(vmem_spec, vmem_spec),
            scratch_shapes=[pltpu.VMEM((n_step, n_keys, rows), BF), pltpu.VMEM((n_keys, rows), F32), acts,
                            head_keys, head_keys, head_keys_t, head_keys_t, acts, acts, acts, flat, acts,
                            pltpu.VMEM((n_step, 8, rows), F32), sums, sums, mid, mid, pair, pair, stage, stage, slim, slim,
                            dma((4,)), dma((n_step,)), dma((1,))] + [dma((n_head - 1,))] * 10 + [dma((3,))] * 4,
            compiler_params=pltpu.CompilerParams(collective_id=1, has_side_effects=True, vmem_limit_bytes=VMEM_MAIN),
            name="attend_out",
        )(q_all, do_own, k_all.reshape(n_keys, HEAD_DIM), v_all.reshape(n_keys, HEAD_DIM), w_q, w_k, w_v, w_o)
        return y_loc, dx_loc

    return jax.shard_map(local_body, mesh=mesh,
                         in_specs=(row_spec, row_spec, full_spec, full_spec, full_spec, full_spec),
                         out_specs=(row_spec, row_spec), check_vma=False)
```

time: 212 us -> 169 us (0.80)
  Pallas kernels: 206 us -> 164 us
    pallas_call x2 -> x1, Pallas kernels: 162 us -> 124 us  [local_body(): pl.pallas_call(functools.partial(main_kernel, n_seq, n_head), out_shape=(...]
    pallas_call x1, Pallas kernels: 44.3 us -> 40.3 us  [local_body(): pl.pallas_call(functools.partial(proj_kernel, n_seq, n_head), out_shape=(...]
where the time goes in v2:
time: 169 us
  Pallas kernels  164 us (97%)
  local copies, waits for them, and re-layouts  4.57 us (3%)
    pallas_call x1, Pallas kernels, local_body(): pl.pallas_call(functools.partial(main_kernel, n_seq, n_head), out_shape=(...  124 us
    pallas_call x1, Pallas kernels, local_body(): pl.pallas_call(functools.partial(proj_kernel, n_seq, n_head), out_shape=(...  40.3 us
    unnamed x2, local copies, waits for them, and re-layouts  4.57 us

profile of v2, /device:TPU:97, one launch (start us, length us, event | category | flops | bytes accessed | tf_op | source)
XLA Modules:
  0.0 169.3 jit_solution(14802853515404788593)
XLA Ops:
  0.6 40.3 %proj_scatter.1 = (bf16[8,128,512]{2,1,0:T(8,128)(2,1)}, bf16[8,128,512]{2,1,0:T(8,128)(2,1)}, bf16[32,128,128]{2,1,0:T(8,128)(2,1)}, bf16[32,128,128]{2,1,0:T(8,128)(2,1)}) custom-call(bf16[128,4096]{1,0:T(8,128)(2,1)} %x_ref.1, bf16[128,4096]{1,0:T(8,128)(2,1)} %dy_ref.1, bf16[4096,4096]{1,0:T(8,128)(2,1)} %wq.3, bf16[4096,1024]{1,0:T(8,128)(2,1)} %wk.3, ...), custom_call_target="tpu_custom_call" | custom-call | tf_op jit(solution)/shard_map/proj_scatter/pallas_call | solution.py:509
  40.9 123.8 %attend_out.1 = (bf16[128,4096]{1,0:T(8,128)(2,1)}, bf16[128,4096]{1,0:T(8,128)(2,1)}) custom-call(bf16[8,128,512]{2,1,0:T(8,128)(2,1)} %get-tuple-element.6.q_in, bf16[8,128,512]{2,1,0:T(8,128)(2,1)} %get-tuple-element.7.do_in, bf16[4096,128]{1,0:T(8,128)(2,1)} %bitcast.2, bf16[4096,128]{1,0:T(8,128)(2,1)} %bitcast.3, bf16[4096,4096]{1,0:T(8,128)(2,1)} %wq.3, ...), custom_call_target="tpu_custom_call" | custom-call | tf_op jit(solution)/shard_map/attend_out/pallas_call | solution.py:535
  164.7 2.3 %copy.10 = bf16[128,4096]{1,0:T(8,128)(2,1)} copy(bf16[128,4096]{1,0:T(8,128)(2,1)} %get-tuple-element.12) | data formatting | bytes 2097152
  167.0 2.3 %copy.11 = bf16[128,4096]{1,0:T(8,128)(2,1)} copy(bf16[128,4096]{1,0:T(8,128)(2,1)} %get-tuple-element.13) | data formatting | bytes 2097152

commit v3 on v2

--- a/solution.py
+++ b/solution.py
@@ -12,6 +12,9 @@
 N_SLOT = 4
 BQ_ROWS = 512
 UC_ROWS = 512
+SCORE_ROWS = 2048
+EXP_ROWS = 1024
+SUB_ROWS = 256
 VMEM_BYTES = 62 * 1024 * 1024
 VMEM_MAIN = 67000000
 MESH_ID = pl.DeviceIdType.MESH
@@ -129,12 +132,21 @@
 
     relays = ((k_out, ky_send, ky_recv, ahead), (v_out, vy_send, vy_recv, behind))
 
-    def forward():
-        for out, send, recv, off in relays:
-            seq_copy(out, send, recv, 0, n_seq - off, off).wait_recv()
-            seq_copy(out, send, recv, 2, n_seq - off, off).start()
-
-    relay_step = n_head // 2
+    def relay(which):
+        out, send, recv, off = relays[which]
+        stage, x_send, x_recv = ((k_st, k_send, k_recv), (v_st, v_send, v_recv))[which]
+        for place in range(1, n_head):
+            row_copy(stage, out, x_send, x_recv, place, seq_id * n_head).wait_recv()
+        pltpu.make_async_copy(stage.at[head_id], out.at[me], loc_sem.at[which]).wait()
+        seq_copy(out, send, recv, 0, 0, off).start()
+        seq_copy(out, send, recv, 1, 0, n_seq - off).start()
+
+    def forward(which):
+        out, send, recv, off = relays[which]
+        seq_copy(out, send, recv, 0, n_seq - off, off).wait_recv()
+        seq_copy(out, send, recv, 2, n_seq - off, off).start()
+
+    relay_steps = (n_head // 4 - 1, (3 * n_head) // 8)
 
     def q_step(step, carry):
         q_tile(step).wait()
@@ -155,15 +167,10 @@
         def _():
             o_tile(step + n_pre - n_head).start()
 
-        @pl.when(step == relay_step)
-        def _():
-            for stage, out, send, recv, loc in ((k_st, k_out, k_send, k_recv, 0), (v_st, v_out, v_send, v_recv, 1)):
-                for off in range(1, n_head):
-                    row_copy(stage, out, send, recv, off, seq_id * n_head).wait_recv()
-                pltpu.make_async_copy(stage.at[head_id], out.at[me], loc_sem.at[loc]).wait()
-            for out, send, recv, off in relays:
-                seq_copy(out, send, recv, 0, 0, off).start()
-                seq_copy(out, send, recv, 1, 0, n_seq - off).start()
+        for which in range(2):
+            @pl.when(step == relay_steps[which])
+            def _():
+                relay(which)
 
         slot = lax.rem(step + 2 * n_kv, N_SLOT)
         q_st[dest(step)] = mm(x_ref[...], wbuf[slot]).astype(BF)
@@ -171,7 +178,7 @@
 
     lax.fori_loop(0, n_head, q_step, 0)
 
-    forward_step = (5 * n_head) // 8
+    forward_steps = (0, n_head // 4)
 
     def do_step(step, carry):
         o_tile(step).wait()
@@ -180,9 +187,10 @@
         def _():
             send_piece(q_st, q_out, q_send, q_recv, 2, n_head - 1)
 
-        @pl.when(step == forward_step)
-        def _():
-            forward()
+        for which in range(2):
+            @pl.when(step == forward_steps[which])
+            def _():
+                forward(which)
 
         @pl.when(step + n_pre < n_head)
         def _():
@@ -223,6 +231,7 @@
     n_tile = y_ref.shape[1] // tile
     blk = min(UC_ROWS, n_keys // n_seq)
     n_chunk = n_keys // blk
+    sub = SUB_ROWS
     part_keys = n_keys // n_seq
     scale = HEAD_DIM ** -0.5
     gain = scale * LOG2E
@@ -273,30 +282,34 @@
         q_blk = read_block(q_vm, step)
 
         def score(i, top):
-            part = aligned(i * blk, blk)
-            s = mm(k_vm[part, :], q_blk, NT)
-            s_buf[part, :] = s
-            return jnp.maximum(top, jnp.max(s.reshape(blk // 8, 8, rows), axis=0))
-
-        top = lax.fori_loop(0, n_chunk, score, jnp.full((8, rows), -jnp.inf, F32))
+            for u in range(SCORE_ROWS // sub):
+                part = aligned(i * SCORE_ROWS + u * sub, sub)
+                s = mm(k_vm[part, :], q_blk, NT)
+                s_buf[part, :] = s
+                top = jnp.maximum(top, jnp.max(s.reshape(sub // 8, 8, rows), axis=0))
+            return top
+
+        top = lax.fori_loop(0, n_keys // SCORE_ROWS, score, jnp.full((8, rows), -jnp.inf, F32))
         top = jnp.max(top, axis=0, keepdims=True)
 
         def expo(i, tot):
-            part = aligned(i * blk, blk)
-            e = jnp.exp2((s_buf[part, :] - top) * gain)
-            s_buf[part, :] = e
-            return tot + jnp.sum(e.reshape(blk // 8, 8, rows), axis=0)
-
-        tot = lax.fori_loop(0, n_chunk, expo, jnp.zeros((8, rows), F32))
+            for u in range(EXP_ROWS // sub):
+                part = aligned(i * EXP_ROWS + u * sub, sub)
+                e = jnp.exp2((s_buf[part, :] - top) * gain)
+                s_buf[part, :] = e
+                tot = tot + jnp.sum(e.reshape(sub // 8, 8, rows), axis=0)
+            return tot
+
+        tot = lax.fori_loop(0, n_keys // EXP_ROWS, expo, jnp.zeros((8, rows), F32))
         inv = 1.0 / jnp.sum(tot, axis=0, keepdims=True)
 
-        def value(i, acc):
-            part = aligned(i * blk, blk)
+        out_t = None
+        for u in range(n_keys // sub):
+            part = pl.ds(u * sub, sub)
             p = (s_buf[part, :] * inv).astype(BF)
             p_all[step, part, :] = p
-            return acc + mm(vt[:, part], p)
-
-        out_t = lax.fori_loop(0, n_chunk, value, jnp.zeros((HEAD_DIM, rows), F32))
+            one = mm(vt[:, part], p)
+            out_t = one if out_t is None else out_t + one
         srcs, cols = block_of(step)
         o_vm[srcs, :, cols] = out_t.T.astype(BF).reshape(n_src, n_rows, HEAD_DIM)
         return carry
@@ -489,6 +502,21 @@
         row_copy(v_st, dv_full.at[:, slim], v_send, v_recv, off).wait_send()
 
 
+def copy_kernel(n_cut, y_in, dx_in, y_out, dx_out, buf, in_sem, out_sem):
+    rows = y_in.shape[0] // n_cut
+    cuts = [(src, dst, slot, pl.ds(cut * rows, rows), slot * n_cut + cut)
+            for cut in range(n_cut) for slot, (src, dst) in enumerate(((y_in, y_out), (dx_in, dx_out)))]
+    ins = [pltpu.make_async_copy(src.at[part], buf.at[slot, part], in_sem.at[sem]) for src, dst, slot, part, sem in cuts]
+    outs = [pltpu.make_async_copy(buf.at[slot, part], dst.at[part], out_sem.at[sem]) for src, dst, slot, part, sem in cuts]
+    for copy in ins:
+        copy.start()
+    for copy, later in zip(ins, outs):
+        copy.wait()
+        later.start()
+    for copy in outs:
+        copy.wait()
+
+
 def solution(mesh):
     n_group = mesh.shape["cp"]
     row_spec = P(("dp", "cp"), None)
@@ -544,7 +572,15 @@
             compiler_params=pltpu.CompilerParams(collective_id=1, has_side_effects=True, vmem_limit_bytes=VMEM_MAIN),
             name="attend_out",
         )(q_all, do_own, k_all.reshape(n_keys, HEAD_DIM), v_all.reshape(n_keys, HEAD_DIM), w_q, w_k, w_v, w_o)
-        return y_loc, dx_loc
+        n_cut = 4
+        return pl.pallas_call(
+            functools.partial(copy_kernel, n_cut),
+            out_shape=(jax.ShapeDtypeStruct((n_rows, n_model), BF), jax.ShapeDtypeStruct((n_rows, n_model), BF)),
+            in_specs=[any_spec] * 2,
+            out_specs=(any_spec, any_spec),
+            scratch_shapes=[pltpu.VMEM((2, n_rows, n_model), BF), dma((2 * n_cut,)), dma((2 * n_cut,))],
+            name="copy_out",
+        )(y_loc, dx_loc)
 
     return jax.shard_map(local_body, mesh=mesh,
                          in_specs=(row_spec, row_spec, full_spec, full_spec, full_spec, full_spec),

time: 169 us -> 149 us (0.88)
  Pallas kernels: 164 us -> 148 us
  local copies, waits for them, and re-layouts: 4.57 us -> 0 us
    pallas_call x1, Pallas kernels: 124 us -> 106 us  [local_body(): pl.pallas_call(functools.partial(main_kernel, n_seq, n_head), out_shape=(...]
    unnamed x2 -> x0, local copies, waits for them, and re-layouts: 4.57 us -> none
    pallas_call x0 -> x1, Pallas kernels: none -> 2.39 us  [local_body(): pl.pallas_call(functools.partial(copy_kernel, n_cut), out_shape=(jax.Shap...]
where the time goes in v3:
time: 149 us
  Pallas kernels  148 us (99%)
    pallas_call x1, Pallas kernels, local_body(): pl.pallas_call(functools.partial(main_kernel, n_seq, n_head), out_shape=(...  106 us
    pallas_call x1, Pallas kernels, local_body(): pl.pallas_call(functools.partial(proj_kernel, n_seq, n_head), out_shape=(...  39.1 us

profile of v3, /device:TPU:97, one launch (start us, length us, event | category | flops | bytes accessed | tf_op | source)
XLA Modules:
  0.0 148.6 jit_solution(6570751645460089046)
XLA Ops:
  0.6 39.1 %proj_scatter.1 = (bf16[8,128,512]{2,1,0:T(8,128)(2,1)}, bf16[8,128,512]{2,1,0:T(8,128)(2,1)}, bf16[32,128,128]{2,1,0:T(8,128)(2,1)}, bf16[32,128,128]{2,1,0:T(8,128)(2,1)}) custom-call(bf16[128,4096]{1,0:T(8,128)(2,1)} %x_ref.1, bf16[128,4096]{1,0:T(8,128)(2,1)} %dy_ref.1, bf16[4096,4096]{1,0:T(8,128)(2,1)} %wq.3, bf16[4096,1024]{1,0:T(8,128)(2,1)} %wk.3, ...), custom_call_target="tpu_custom_call" | custom-call | tf_op jit(solution)/shard_map/proj_scatter/pallas_call | solution.py:537
  39.7 106.3 %attend_out.1 = (bf16[128,4096]{1,0:T(8,128)(2,1)}, bf16[128,4096]{1,0:T(8,128)(2,1)}) custom-call(bf16[8,128,512]{2,1,0:T(8,128)(2,1)} %get-tuple-element.8.q_in, bf16[8,128,512]{2,1,0:T(8,128)(2,1)} %get-tuple-element.9.do_in, bf16[4096,128]{1,0:T(8,128)(2,1)} %bitcast.2, bf16[4096,128]{1,0:T(8,128)(2,1)} %bitcast.3, bf16[4096,4096]{1,0:T(8,128)(2,1)} %wq.3, ...), custom_call_target="tpu_custom_call" | custom-call | tf_op jit(solution)/shard_map/attend_out/pallas_call | solution.py:563
  146.0 2.4 %copy_out.1 = (bf16[128,4096]{1,0:T(8,128)(2,1)}, bf16[128,4096]{1,0:T(8,128)(2,1)}) custom-call(bf16[128,4096]{1,0:T(8,128)(2,1)} %get-tuple-element.12.y_in, bf16[128,4096]{1,0:T(8,128)(2,1)} %get-tuple-element.13.dx_in), custom_call_target="tpu_custom_call" | custom-call | tf_op jit(solution)/shard_map/copy_out/pallas_call | solution.py:576
